TPU v7x, 256 devices: a whole 4x4x8 slice. The times are simulated.
256 devices in a mesh: dp: 32 (over z, y), vp: 8 (over x, core).
Axes of the slice: x: 4, y: 4, z: 8, core: 2. Of those that a mesh axis runs over, the one named last changes fastest.
Arguments:
- hidden: bfloat16 [96, 128, 896], P('dp')
- norm_gain: float32 [896], replicated
- emb_table: bfloat16 [151936, 896], P('vp')
- labels: int32 [96, 128], P('dp')
- tok_mask: float32 [96, 128], P('dp')
Outputs:
- output 1: float32 [], replicated
- output 2: float32 [151936, 896], P('vp')
- output 3: bfloat16 [96, 128, 896], P('dp')
- output 4: float32 [896], replicated
All inputs are finite; a program needn't handle non-finite values.
Results may differ from a plain program's by a relative error of at most 0.001.
Values sent between devices are 32-bit elements.
A program may use at most 768 MiB of HBM per device.

v0:
```python
import jax
import jax.numpy as jnp
from jax import lax
from jax.sharding import PartitionSpec as P

LOGIT_SCALE = 0.0625
EPS = 1e-5


def norm_forward(tokens, norm_gain):
    values = tokens.astype(jnp.float32)
    mean_x = jnp.mean(values, axis=-1, keepdims=True)
    centered = values - mean_x
    variance = jnp.mean(centered * centered, axis=-1, keepdims=True)
    inv_std = lax.rsqrt(variance + EPS)
    x_hat = centered * inv_std
    return (norm_gain * x_hat).astype(jnp.bfloat16), x_hat, inv_std


def norm_backward(d_normed, x_hat, inv_std, norm_gain):
    value_a6 = d_normed * norm_gain
    mean_one = jnp.mean(value_a6, axis=-1, keepdims=True)
    mean_two = jnp.mean(value_a6 * x_hat, axis=-1, keepdims=True)
    return (inv_std * (value_a6 - mean_one - x_hat * mean_two)).astype(jnp.bfloat16)


def solution(mesh):
    def local_step(hidden, norm_gain, emb_table, labels, tok_mask):
        rows, seq_len, width = hidden.shape
        vocab_local = emb_table.shape[0]
        flat_labels = labels.reshape(-1)
        flat_mask = tok_mask.reshape(-1)
        normed, x_hat, inv_std = norm_forward(hidden.reshape(rows * seq_len, width), norm_gain)
        logits = LOGIT_SCALE * jnp.einsum('td,vd->tv', normed, emb_table, preferred_element_type=jnp.float32)
        row_max = lax.pmax(jnp.max(logits, axis=1), 'vp')
        shifted = jnp.exp(logits - row_max[:, None])
        exp_sum = lax.psum(jnp.sum(shifted, axis=1), 'vp')
        log_norm = row_max + jnp.log(exp_sum)
        local_ids = flat_labels - lax.axis_index('vp') * vocab_local
        hits = jnp.arange(vocab_local)[None, :] == local_ids[:, None]
        label_logit = lax.psum(jnp.sum(jnp.where(hits, logits, 0.0), axis=1), 'vp')
        count = lax.psum(jnp.sum(flat_mask), 'dp')
        loss_sum = lax.psum(jnp.sum(flat_mask * (log_norm - label_logit)), 'dp')
        soft_probs = shifted * (1.0 / exp_sum)[:, None]
        weight = flat_mask * (LOGIT_SCALE / count)
        d_logits = (jnp.where(hits, soft_probs - 1.0, soft_probs) * weight[:, None]).astype(jnp.bfloat16)
        d_normed = lax.psum(jnp.dot(d_logits, emb_table, preferred_element_type=jnp.float32), 'vp')
        table_grad = lax.psum(jnp.einsum('tv,td->vd', d_logits, normed, preferred_element_type=jnp.float32), 'dp')
        gain_grad = lax.psum(jnp.sum(d_normed * x_hat, axis=0), 'dp')
        d_tokens = norm_backward(d_normed, x_hat, inv_std, norm_gain)
        return loss_sum / count, table_grad, d_tokens.reshape(rows, seq_len, width), gain_grad

    return jax.shard_map(local_step, mesh=mesh, in_specs=(P('dp', None, None), P(None), P('vp', None), P('dp', None), P('dp', None)), out_specs=(P(), P('vp', None), P('dp', None, None), P(None)), check_vma=False)
```

profile of v0, /device:TPU:1, one launch (start us, length us, event | category | flops | bytes accessed | tf_op | source)
XLA Modules:
  0.0 1371.0 jit_solution(1388954075108359976)
XLA Ops:
  7.2 0.0 all-reduce.7.cloned.1.call-start
  7.2 1.3 reduce_sum.86
  8.5 65.2 %psum.52 = f32[]{:T(128)} all-reduce(f32[]{:T(128)} %reduce_sum.86), channel_id=1, replica_groups=mesh['dp'=32,'vp'=8] {'dp'}, use_global_device_ids=true, to_apply=%region_11.12 | all-reduce | flops 1 | bytes 8 | tf_op jit(solution)/shard_map/psum | solution.py:42
  73.7 1.3 convert_reduce_fusion
  75.0 1.4 multiply_reduce_fusion.2
  76.4 1.4 multiply_convert_fusion.1
  77.8 0.0 copy-start.3
  77.8 29.2 %fusion.10 = (f32[384]{0:T(512)S(1)}, f32[384,18992]{0,1:T(8,128)}) fusion(bf16[384,896]{1,0:T(8,128)(2,1)S(1)} %multiply_convert_fusion.1, bf16[18992,896]{1,0:T(8,128)(2,1)} %param.7), kind=kOutput, calls=%fused_computation.29 | convolution fusion | flops 13083512832 | bytes 63895040 | tf_op jit(solution)/shard_map/td,vd->tv/dot_general | solution.py:34
  107.0 26.8 %pmax.7 = f32[384]{0:T(512)S(1)} all-reduce(f32[384]{0:T(512)S(1)} %get-tuple-element.18), channel_id=1, replica_groups=mesh['dp'=32,'vp'=8] {'vp'}, use_global_device_ids=true, to_apply=%region_3.0 | all-reduce | flops 384 | bytes 3072 | tf_op jit(solution)/shard_map/pmax | solution.py:35
  134.5 13.5 fusion.2
  148.0 12.6 all-reduce.1
  160.6 0.6 broadcast_divide_fusion
  161.2 26.0 %fusion.6 = f32[384,896]{1,0:T(8,128)} fusion(bf16[18992,896]{1,0:T(8,128)(2,1)} %param.7, f32[384,18992]{0,1:T(8,128)} %get-tuple-element.19, f32[384]{0:T(512)S(1)} %get-tuple-element.15, f32[384]{0:T(512)S(1)} %get-tuple-element.13, s32[384]{0:T(512)S(1)} %subtract_bitcast_fusion, f32[384]{0:T(512)S(1)} %pmax.7), kind=kOutput, calls=%fused_computation.27 | convolution fusion | flops 13119977472 | bytes 64587776 | tf_op jit(solution)/shard_map/dot_general | solution.py:47
  187.2 0.0 all-reduce.7.cloned.1.call-update
  187.2 0.0 all-reduce.5.cloned.1.call-start
  187.3 37.2 %fusion.8 = f32[18992,896]{1,0:T(8,128)} fusion(bf16[384,896]{1,0:T(8,128)(2,1)S(1)} %multiply_convert_fusion.1, f32[384,18992]{0,1:T(8,128)} %get-tuple-element.19, f32[384]{0:T(512)S(1)} %get-tuple-element.15, f32[384]{0:T(512)S(1)} %get-tuple-element.13, s32[384]{0:T(512)S(1)} %subtract_bitcast_fusion, f32[384]{0:T(512)S(1)} %pmax.7), kind=kOutput, calls=%fused_computation.28 | convolution fusion | flops 13119977472 | bytes 97933312 | tf_op jit(solution)/shard_map/tv,td->vd/dot_general | solution.py:48
  224.5 0.0 all-reduce.5.cloned.1.call-update
  224.5 21.4 %all-reduce.7.cloned.1.call-done = f32[384,896]{1,0:T(8,128)} async-done(((f32[384,896]{1,0:T(8,128)}), f32[384,896]{1,0:T(8,128)}) %all-reduce.7.cloned.1.call-update) | async-done | bytes 1376272 | tf_op jit(solution)/shard_map/psum | solution.py:47
  246.0 0.0 copy-done.1
  246.0 2.0 multiply_reduce_fusion
  248.0 65.3 %all-reduce = (f32[]{:T(128)}, f32[896]{0:T(1024)}) all-reduce(f32[]{:T(128)} %get-tuple-element.14, f32[896]{0:T(1024)S(1)} %get-tuple-element.6), channel_id=1, replica_groups=mesh['dp'=32,'vp'=8] {'dp'}, use_global_device_ids=true, to_apply=%region_9.10 | all-reduce | flops 897 | bytes 7176 | tf_op jit(solution)/shard_map/psum | solution.py:43
  314.6 2.6 multiply_convert_fusion
  317.3 1002.0 %all-reduce.5.cloned.1.call-done = f32[18992,896]{1,0:T(8,128)} async-done(((f32[18992,896]{1,0:T(8,128)}), f32[18992,896]{1,0:T(8,128)}) %all-reduce.5.cloned.1.call-update) | async-done | bytes 68067344 | tf_op jit(solution)/shard_map/psum | solution.py:48
  1319.2 43.8 %copy.11 = f32[18992,896]{1,0:T(8,128)} copy(f32[18992,896]{1,0:T(8,128)} %all-reduce.5.cloned.1.call-done) | data formatting | bytes 136134656
  (10 shorter events, 0.0 us)
Async XLA Ops:
  7.2 238.8 %all-reduce.7.cloned.1.call-start = ((), (), s32[]{:S(2)}) async-start(), calls=%async_computation.1 | async-start | bytes 2752512 | tf_op jit(solution)/shard_map/psum | solution.py:47
  77.8 56.7 %copy-start.3 = (s32[3,128]{1,0:T(4,128)S(1)}, s32[3,128]{1,0:T(4,128)}, u32[]{:S(2)}) copy-start(s32[3,128]{1,0:T(4,128)} %param.8) | copy-start | bytes 4612
  107.0 53.6 %copy-start.2 = (f32[3,128]{1,0:T(4,128)S(1)}, f32[3,128]{1,0:T(4,128)}, u32[]{:S(2)}) copy-start(f32[3,128]{1,0:T(4,128)} %param.9) | copy-start | bytes 4612
  187.2 1132.0 %all-reduce.5.cloned.1.call-start = ((), (), s32[]{:S(2)}) async-start(), calls=%async_computation | async-start | bytes 136134656 | tf_op jit(solution)/shard_map/psum | solution.py:48
  224.5 21.5 %copy-start = (bf16[3,128,896]{2,1,0:T(8,128)(2,1)S(1)}, bf16[3,128,896]{2,1,0:T(8,128)(2,1)}, u32[]{:S(2)}) copy-start(bf16[3,128,896]{2,1,0:T(8,128)(2,1)} %param.5) | copy-start | bytes 2064388
  224.5 21.5 %copy-start.1 = (f32[896]{0:T(1024)S(1)}, f32[896]{0:T(1024)}, u32[]{:S(2)}) copy-start(f32[896]{0:T(1024)} %param.6) | copy-start | bytes 10756
Sparse Core Ops, SparseCore 0:
  187.3 58.5 all-reduce.6
  250.7 1068.4 all-reduce.4
where the time goes:
time: 1370 us
  waiting for transfers between devices  1020 us (74%)
  blocking collectives  170 us (12%)
  matrix products  92.5 us (7%)
  local copies, waits for them, and re-layouts  43.9 us (3%)
  other arithmetic  24.1 us (2%)
  between operations  17.3 us (1%)
    psum x1, waiting for transfers between devices, local_step(): lax.psum(jnp.einsum('tv,td->vd', d_logits, normed, preferred_element_type...  1000 us
    psum x1, blocking collectives, local_step(): loss_sum = lax.psum(jnp.sum(flat_mask * (log_norm - label_logit)), 'dp')  65.3 us
    psum x1, blocking collectives, local_step(): count = lax.psum(jnp.sum(flat_mask), 'dp')  65.2 us
    unnamed x9, local copies, waits for them, and re-layouts  43.9 us
    dot_general x1, matrix products, local_step(): jnp.einsum('tv,td->vd', d_logits, normed, preferred_element_type=jnp.floa...  37.2 us
    dot_general x1, matrix products, local_step(): jnp.einsum('td,vd->tv', normed, emb_table, preferred_element_type=jnp.flo...  29.2 us
  transfers between devices with their start and end apart: 2, of which 2 were waited for; matrix products, arithmetic and copies ran while one was open for 3% of the time, Pallas kernels for 0%

commit v1 on v0

v1 whole, which is shorter than its diff:
```python
import functools
import heapq

import jax
import jax.numpy as jnp
from jax import lax
from jax.experimental import pallas as pl
from jax.experimental.pallas import tpu as pltpu
from jax.sharding import PartitionSpec as P

MESH = pl.DeviceIdType.MESH
LOGIT_SCALE = 0.0625
EPS = 1e-5
NZ, NY, NV = 8, 4, 8
NDP = NZ * NY
TOK = 384
WIDTH = 896
VLOC = 18992
NALL = NDP * TOK
SPLIT = 160
COLOR_ROWS = 2304
CHUNK = 192
HALF = CHUNK // 2
NCHUNK = COLOR_ROWS // CHUNK
B_BASE = 4 * COLOR_ROWS
REST_BASE = 8 * COLOR_ROWS
REST_PARTS = ((REST_BASE, 288), (REST_BASE + 288, VLOC - REST_BASE - 288))
SLOTS = 3
TT = 2048
NT = NALL // TT
VT = 1200
NVT = -(-VLOC // VT)
SLICE = TOK // NV
F32 = jnp.float32
BF16 = jnp.bfloat16
VMEM_LIMIT = 63 * 2**20


def dot_nt(a, b):
    return lax.dot_general(a, b, (((1,), (1,)), ((), ())), preferred_element_type=F32)


def rsqrt_norm(values):
    mean_x = jnp.mean(values, axis=-1, keepdims=True)
    centered = values - mean_x
    variance = jnp.mean(centered * centered, axis=-1, keepdims=True)
    inv_std = lax.rsqrt(variance + EPS)
    return centered * inv_std, inv_std


def row_start(i):
    return pl.multiple_of(jnp.minimum(i * VT, VLOC - VT), 16)


def stats_kernel(vp_ref, hid_ref, gain_ref, lab_ref, mask_ref, emb_ref, nf_ref, st_ref, nb, m_s, s_s, l_s):
    i = pl.program_id(0)

    @pl.when(i == 0)
    def _():
        x_hat, _ = rsqrt_norm(hid_ref[...].astype(F32))
        normed = (gain_ref[...] * x_hat).astype(BF16)
        nb[...] = normed
        nf_ref[...] = normed.astype(F32)
        m_s[...] = jnp.full_like(m_s, -jnp.inf)
        s_s[...] = jnp.zeros_like(s_s)
        l_s[...] = jnp.zeros_like(l_s)

    logits = LOGIT_SCALE * dot_nt(emb_ref[...], nb[...])
    ids = lax.broadcasted_iota(jnp.int32, (VT, TOK), 0) + row_start(i)
    hit = ids == lab_ref[...] - vp_ref[0] * VLOC
    fresh = ids >= i * VT
    masked = jnp.where(fresh, logits, -jnp.inf).reshape(VT // 8, 8, TOK)
    top = jnp.maximum(m_s[...], jnp.max(masked, axis=0))
    s_s[...] = s_s[...] * jnp.exp(m_s[...] - top) + jnp.sum(jnp.exp(masked - top[None]), axis=0)
    m_s[...] = top
    picked = jnp.where(jnp.logical_and(hit, fresh), logits, 0.0).reshape(VT // 8, 8, TOK)
    l_s[...] += jnp.sum(picked, axis=0)

    @pl.when(i == pl.num_programs(0) - 1)
    def _():
        row_m = jnp.max(m_s[...], axis=0, keepdims=True)
        row_s = jnp.sum(s_s[...] * jnp.exp(m_s[...] - row_m), axis=0, keepdims=True)
        row_l = jnp.sum(l_s[...], axis=0, keepdims=True)
        zeros = jnp.zeros((3, TOK), F32)
        st_ref[...] = jnp.concatenate([row_m, row_s, row_l, mask_ref[...], lab_ref[...].astype(F32), zeros], axis=0)


def own_stats(vp, hidden, gain, labels, mask, emb):
    whole = lambda shape: pl.BlockSpec(shape, lambda i, v: (0,) * len(shape))
    return pl.pallas_call(
        stats_kernel,
        grid_spec=pltpu.PrefetchScalarGridSpec(
            num_scalar_prefetch=1,
            grid=(NVT,),
            in_specs=[
                whole((TOK, WIDTH)),
                whole((1, WIDTH)),
                whole((1, TOK)),
                whole((1, TOK)),
                pl.BlockSpec((pl.Element(VT), pl.Element(WIDTH)), lambda i, v: (row_start(i), 0)),
            ],
            out_specs=[whole((TOK, WIDTH)), whole((8, TOK))],
            scratch_shapes=[pltpu.VMEM((TOK, WIDTH), BF16)] + [pltpu.VMEM((8, TOK), F32)] * 3,
        ),
        out_shape=[jax.ShapeDtypeStruct((TOK, WIDTH), F32), jax.ShapeDtypeStruct((8, TOK), F32)],
        compiler_params=pltpu.CompilerParams(dimension_semantics=("arbitrary",), vmem_limit_bytes=VMEM_LIMIT),
        name="own_stats",
    )(vp, hidden, gain, labels, mask, emb)


STEP = {"z+": (1, 0), "z-": (-1, 0), "y+": (0, 1), "y-": (0, -1)}


def tree_first():
    lo, mid, hi = 0, SPLIT // 2, SPLIT
    msgs = [
        dict(a=0, b=1, lo=lo, hi=hi, link="y+", parents=[]),
        dict(a=0, b=-1, lo=lo, hi=hi, link="y-", parents=[]),
        dict(a=0, b=2, lo=lo, hi=mid, link="y+", parents=[0]),
        dict(a=0, b=-2, lo=mid, hi=hi, link="y-", parents=[1]),
    ]
    for sign, link, part in ((1, "z+", (0, 2)), (-1, "z-", (2, 2))):
        for s in (1, 2, 3, 4):
            parents = [0, 1, 2, 3] if s == 1 else [len(msgs) - 1]
            msgs.append(dict(a=sign * s, b=(0, 4) if s < 4 else part, lo=lo, hi=hi, link=link, parents=parents))
    return msgs


def tree_second():
    lo, mid, hi = SPLIT, (SPLIT + TOK) // 2, TOK
    msgs = []
    nodes = [(0, lo, hi, None)]
    for sign, link, half in ((1, "z+", (lo, mid)), (-1, "z-", (mid, hi))):
        for s in (1, 2, 3, 4):
            rows = (lo, hi) if s < 4 else half
            parents = [] if s == 1 else [len(msgs) - 1]
            msgs.append(dict(a=sign * s, b=0, lo=rows[0], hi=rows[1], link=link, parents=parents))
            nodes.append((sign * s, rows[0], rows[1], len(msgs) - 1))
    for a, first, last, node in nodes:
        parents = [] if node is None else [node]
        up, down = len(msgs), len(msgs) + 1
        msgs.append(dict(a=a, b=1, lo=first, hi=last, link="y+", parents=parents))
        msgs.append(dict(a=a, b=-1, lo=first, hi=last, link="y-", parents=parents))
        if abs(a) < 4:
            msgs.append(dict(a=a, b=2, lo=lo, hi=mid, link="y+", parents=[up]))
            msgs.append(dict(a=a, b=-2, lo=mid, hi=hi, link="y-", parents=[down]))
        elif a == 4:
            msgs.append(dict(a=a, b=2, lo=first, hi=last, link="y+", parents=[up]))
        else:
            msgs.append(dict(a=a, b=-2, lo=first, hi=last, link="y-", parents=[down]))
    return msgs


def arrival_order(msgs):
    size = lambda m: (m["hi"] - m["lo"]) * (m["b"][1] if isinstance(m["b"], tuple) else 1)
    free = {link: 0.0 for link in STEP}
    waiting = {i: set(m["parents"]) for i, m in enumerate(msgs)}
    heap, order = [], []

    def push(i, now):
        link = msgs[i]["link"]
        free[link] = max(free[link], now) + size(msgs[i]) * WIDTH * 4 / 60e3
        heapq.heappush(heap, (free[link] + 2.0, i))

    for i in range(len(msgs)):
        if not waiting[i]:
            push(i, 0.0)
    while heap:
        now, i = heapq.heappop(heap)
        order.append(i)
        for j in range(len(msgs)):
            if i in waiting[j]:
                waiting[j].discard(i)
                if not waiting[j]:
                    push(j, now)
    return order


FIRST, SECOND = tree_first(), tree_second()
NMSG = max(len(FIRST), len(SECOND))


def peers():
    dp, vp = lax.axis_index("dp"), lax.axis_index("vp")
    z, y = lax.div(dp, NY), lax.rem(dp, NY)
    ys = [z * NY + lax.rem(y + d, NY) for d in range(1, NY)]
    zs = [lax.rem(z + d, NZ) * NY + y for d in range(1, NZ)]
    vs = [lax.rem(vp + d, NV) for d in range(1, NV)]
    return dp, vp, z, y, ys, zs, vs


def greet(dp, vp, ys, zs, vs):
    barrier = pltpu.get_barrier_semaphore()
    everyone = [(d, vp) for d in ys + zs] + [(dp, v) for v in vs]
    for device in everyone:
        pl.semaphore_signal(barrier, inc=1, device_id=device, device_id_type=MESH)
    pl.semaphore_wait(barrier, len(everyone))


def remote(src, dst, send, recv, device):
    return pltpu.make_async_remote_copy(
        src_ref=src, dst_ref=dst, send_sem=send, recv_sem=recv, device_id=device, device_id_type=MESH
    )


def gather_kernel(nf_ref, st_ref, nall_ref, stall_ref, vbuf, stbuf, local, sent, got, twin, st_sent, st_got):
    dp, vp, z, y, ys, zs, vs = peers()
    core = lax.rem(vp, 2)
    other = vp + 1 - 2 * core
    greet(dp, vp, ys, zs, vs)

    def region(m, dz=0, dy=0):
        zz = lax.rem(z - m["a"] + dz + 2 * NZ, NZ)
        rows = pl.ds(m["lo"], m["hi"] - m["lo"])
        if isinstance(m["b"], tuple):
            return nall_ref.at[zz, pl.ds(*m["b"]), rows]
        return nall_ref.at[zz, lax.rem(y - m["b"] + dy + 2 * NY, NY), rows]

    def target(link, back=False):
        dz, dy = STEP[link]
        if back:
            dz, dy = -dz, -dy
        return (lax.rem(z + dz + NZ, NZ) * NY + lax.rem(y + dy + NY, NY), vp)

    def send(m, i, mine):
        dz, dy = STEP[m["link"]]
        place = region(m, dz, dy)
        src = nf_ref.at[pl.ds(m["lo"], m["hi"] - m["lo"])] if mine else place
        copy = remote(src, place, sent.at[i], got.at[i], target(m["link"]))
        copy.start()
        return copy

    own = pltpu.make_async_copy(nf_ref, nall_ref.at[z, y], local)
    own.start()
    for which, msgs in ((0, FIRST), (1, SECOND)):

        @pl.when(core == which)
        def _():
            for i, m in enumerate(msgs):
                if not m["parents"]:
                    send(m, i, True)

    vbuf[vp] = st_ref[...]
    stat_copies = [
        remote(st_ref, vbuf.at[vp], st_sent.at[i], st_got.at[i], (dp, v)) for i, v in enumerate(vs)
    ]
    for copy in stat_copies:
        copy.start()
    for i, v in enumerate(vs):
        source = lax.rem(vp + NV - 1 - i, NV)
        remote(st_ref, vbuf.at[source], st_sent.at[i], st_got.at[i], (dp, v)).wait_recv()
    row_m = vbuf[0, 0:1]
    for p in range(1, NV):
        row_m = jnp.maximum(row_m, vbuf[p, 0:1])
    row_s = jnp.zeros_like(row_m)
    row_l = jnp.zeros_like(row_m)
    for p in range(NV):
        row_s += vbuf[p, 1:2] * jnp.exp(vbuf[p, 0:1] - row_m)
        row_l += vbuf[p, 2:3]
    lse = row_m + jnp.log(row_s)
    lanes = lambda d, n=1: pl.ds(pl.multiple_of(d * TOK, TOK), n * TOK)
    stbuf[:, lanes(dp)] = jnp.concatenate([lse, st_ref[3:5], row_l, jnp.zeros((4, TOK), F32)], axis=0)
    for i, d in enumerate(ys):
        copy = remote(stbuf.at[:, lanes(dp)], stbuf.at[:, lanes(dp)], st_sent.at[7 + i], st_got.at[7 + i], (d, vp))
        copy.start()
        stat_copies.append(copy)
    for i, d in enumerate(ys):
        source = z * NY + lax.rem(y + NY - 1 - i, NY)
        place = stbuf.at[:, lanes(source)]
        remote(place, place, st_sent.at[7 + i], st_got.at[7 + i], (d, vp)).wait_recv()
    for i, d in enumerate(zs):
        place = stbuf.at[:, lanes(z * NY, NY)]
        copy = remote(place, place, st_sent.at[10 + i], st_got.at[10 + i], (d, vp))
        copy.start()
        stat_copies.append(copy)

    own.wait()
    for which, msgs, others in ((0, FIRST, SECOND), (1, SECOND, FIRST)):

        @pl.when(core == which)
        def _():
            ready = set()
            copies = []
            for i, m in enumerate(msgs):
                if not m["parents"]:
                    place = region(m, *STEP[m["link"]])
                    src = nf_ref.at[pl.ds(m["lo"], m["hi"] - m["lo"])]
                    copies.append(remote(src, place, sent.at[i], got.at[i], target(m["link"])))
            for i in arrival_order(msgs):
                m = msgs[i]
                place = region(m)
                remote(place, place, sent.at[i], got.at[i], target(m["link"], True)).wait_recv()
                ready.add(i)
                for j, child in enumerate(msgs):
                    if i in child["parents"] and ready.issuperset(child["parents"]):
                        copies.append(send(child, j, False))
                copy = remote(place, place, sent.at[NMSG + i], twin.at[i], (dp, other))
                copy.start()
                copies.append(copy)
            for i, m in enumerate(others):
                place = region(m)
                remote(place, place, sent.at[i], twin.at[i], (dp, other)).wait_recv()
            for copy in copies:
                copy.wait_send()

    for i, d in enumerate(zs):
        source = lax.rem(z + NZ - 1 - i, NZ)
        place = stbuf.at[:, lanes(source * NY, NY)]
        remote(place, place, st_sent.at[10 + i], st_got.at[10 + i], (d, vp)).wait_recv()
    for copy in stat_copies:
        copy.wait_send()
    stall_ref[...] = stbuf[...]


def gather(nf, st):
    any_space = pl.BlockSpec(memory_space=pl.ANY)
    vmem = pl.BlockSpec(memory_space=pltpu.VMEM)
    return pl.pallas_call(
        gather_kernel,
        in_specs=[vmem, vmem],
        out_specs=[any_space, vmem],
        out_shape=[jax.ShapeDtypeStruct((NZ, NY, TOK, WIDTH), F32), jax.ShapeDtypeStruct((8, NALL), F32)],
        scratch_shapes=[
            pltpu.VMEM((NV, 8, TOK), F32),
            pltpu.VMEM((8, NALL), F32),
            pltpu.SemaphoreType.DMA,
            pltpu.SemaphoreType.DMA((2 * NMSG,)),
            pltpu.SemaphoreType.DMA((NMSG,)),
            pltpu.SemaphoreType.DMA((NMSG,)),
            pltpu.SemaphoreType.DMA((17,)),
            pltpu.SemaphoreType.DMA((17,)),
        ],
        compiler_params=pltpu.CompilerParams(
            collective_id=0, has_side_effects=True, vmem_limit_bytes=VMEM_LIMIT
        ),
        name="gather_tokens",
    )(nf, st)


def weight_scale(st_ref):
    return LOGIT_SCALE / jnp.sum(st_ref[1:2, :])


def dn_kernel(ids_ref, nf_ref, st_ref, own_ref, emb_ref, dn_ref, w_s):
    i = pl.program_id(0)

    @pl.when(i == 0)
    def _():
        w_s[...] = own_ref[1:2, :] * weight_scale(st_ref)
        dn_ref[...] = jnp.zeros_like(dn_ref)

    emb = emb_ref[...]
    logits = LOGIT_SCALE * dot_nt(emb, nf_ref[...].astype(BF16))
    ids = lax.broadcasted_iota(jnp.int32, (VT, TOK), 0) + row_start(i)
    soft = jnp.exp(logits - own_ref[0:1, :])
    hit = ids == own_ref[2:3, :].astype(jnp.int32) - ids_ref[1] * VLOC
    weight = jnp.where(ids >= i * VT, w_s[...], 0.0)
    d_logits = (jnp.where(hit, soft - 1.0, soft) * weight).astype(BF16)
    dn_ref[...] += lax.dot_general(d_logits, emb, (((0,), (0,)), ((), ())), preferred_element_type=F32)


def own_dn(ids, nf, stall, emb):
    whole = lambda shape: pl.BlockSpec(shape, lambda i, v: (0,) * len(shape))
    return pl.pallas_call(
        dn_kernel,
        grid_spec=pltpu.PrefetchScalarGridSpec(
            num_scalar_prefetch=1,
            grid=(NVT,),
            in_specs=[
                whole((TOK, WIDTH)),
                whole((8, NALL)),
                pl.BlockSpec((8, TOK), lambda i, v: (0, v[0])),
                pl.BlockSpec((pl.Element(VT), pl.Element(WIDTH)), lambda i, v: (row_start(i), 0)),
            ],
            out_specs=whole((TOK, WIDTH)),
            scratch_shapes=[pltpu.VMEM((1, TOK), F32)],
        ),
        out_shape=jax.ShapeDtypeStruct((TOK, WIDTH), F32),
        compiler_params=pltpu.CompilerParams(dimension_semantics=("arbitrary",), vmem_limit_bytes=VMEM_LIMIT),
        name="own_dn",
    )(ids, nf, stall, stall, emb)


def table_kernel(
    nall_ref, st_ref, emb_ref, dn_ref, hid_ref, gain_ref, table_ref, dh_ref, dg_ref, loss_ref,
    nb, stage, ebuf, acc, rows, dnbuf, dhbuf, gv, gy, gz,
    stage_sem, e_sem, l_sem, sent, got, v_sent, v_got,
):
    dp, vp, z, y, ys, zs, vs = peers()
    greet(dp, vp, ys, zs, vs)
    color_a = lax.rem(y + 2 * z, 4)
    color_b = lax.rem(z + 2 * y, 4)

    def a_row(color, k, start=0):
        return pl.multiple_of(color * COLOR_ROWS + k * CHUNK + start, HALF)

    def b_row(color, k, start=0):
        return pl.multiple_of(B_BASE + color * COLOR_ROWS + k * CHUNK + start, HALF)

    def fetch_rows(k, slot):
        return [
            pltpu.make_async_copy(
                emb_ref.at[pl.ds(a_row(color_a, k), CHUNK)], ebuf.at[slot, pl.ds(0, CHUNK)], e_sem.at[slot, 0]
            ),
            pltpu.make_async_copy(
                emb_ref.at[pl.ds(b_row(color_b, k), CHUNK)], ebuf.at[slot, pl.ds(CHUNK, CHUNK)], e_sem.at[slot, 1]
            ),
        ]

    def fetch_rest(part, slot):
        start, size = REST_PARTS[part]
        return pltpu.make_async_copy(
            emb_ref.at[pl.ds(start, size)], ebuf.at[slot, pl.ds(0, size)], e_sem.at[slot, 0]
        )

    def fetch_tokens(t, slot):
        return pltpu.make_async_copy(nall_ref.at[pl.ds(t * TT, TT)], stage.at[slot], stage_sem.at[slot])

    for copy in fetch_rows(0, 0):
        copy.start()
    fetch_tokens(0, 0).start()

    def part(v):
        return pl.ds(pl.multiple_of(v * SLICE, SLICE), SLICE)

    def dn_copy(i, v):
        return remote(dn_ref.at[part(v)], dnbuf.at[vp], v_sent.at[i], v_got.at[i], (dp, v))

    for i, v in enumerate(vs):
        dn_copy(i, v).start()

    count = jnp.sum(st_ref[1:2, :])
    rows[0:1] = st_ref[0:1, :]
    rows[1:2] = st_ref[1:2, :] * (LOGIT_SCALE / count)
    rows[2:3] = st_ref[2:3, :] - (vp * VLOC).astype(F32)
    loss_ref[0, 0] = jnp.sum(st_ref[1:2, :] * (st_ref[0:1, :] - st_ref[3:4, :])) / count

    def block(slot, rows_in, t, size, ids):
        tok = pl.ds(pl.multiple_of(t * TT, TT), TT)
        n = nb[tok, :]
        logits = LOGIT_SCALE * dot_nt(ebuf[rows_in, 0:size], n)
        soft = jnp.exp(logits - rows[0:1, tok])
        hit = ids == rows[2:3, tok].astype(jnp.int32)
        d_logits = (jnp.where(hit, soft - 1.0, soft) * rows[1:2, tok]).astype(BF16)
        acc[slot, 0:size] += jnp.dot(d_logits, n, preferred_element_type=F32)

    up_y, down_y = (ys[0], vp), (ys[2], vp)
    up_z, down_z = (zs[0], vp), (zs[6], vp)

    def row_copies(k, slot, ca, cb):
        a0, b0 = 0, CHUNK
        plan = [
            (a0, CHUNK, a_row(ca["y+"], k), up_y),
            (a0, CHUNK, a_row(ca["y-"], k), down_y),
            (a0, HALF, a_row(ca["z+"], k), up_z),
            (a0 + HALF, HALF, a_row(ca["z-"], k, HALF), down_z),
            (b0, CHUNK, b_row(cb["z+"], k), up_z),
            (b0, CHUNK, b_row(cb["z-"], k), down_z),
            (b0, HALF, b_row(cb["y+"], k), up_y),
            (b0 + HALF, HALF, b_row(cb["y-"], k, HALF), down_y),
        ]
        return [
            remote(acc.at[slot, pl.ds(lo, n)], table_ref.at[pl.ds(row, n)], sent.at[slot, i], got.at[k, i], device)
            for i, (lo, n, row, device) in enumerate(plan)
        ]

    def out_copies(k, slot):
        mine_a = dict.fromkeys(STEP, color_a)
        mine_b = dict.fromkeys(STEP, color_b)
        return row_copies(k, slot, mine_a, mine_b)

    def in_copies(k):
        from_a = {"y+": lax.rem(color_a + 3, 4), "y-": lax.rem(color_a + 1, 4)}
        from_a["z+"] = from_a["z-"] = lax.rem(color_a + 2, 4)
        from_b = {"z+": lax.rem(color_b + 3, 4), "z-": lax.rem(color_b + 1, 4)}
        from_b["y+"] = from_b["y-"] = lax.rem(color_b + 2, 4)
        return row_copies(k, 0, from_a, from_b)

    def keep_copies(k, slot):
        return [
            pltpu.make_async_copy(
                acc.at[slot, pl.ds(0, CHUNK)], table_ref.at[pl.ds(a_row(color_a, k), CHUNK)], l_sem.at[slot, 0]
            ),
            pltpu.make_async_copy(
                acc.at[slot, pl.ds(CHUNK, CHUNK)], table_ref.at[pl.ds(b_row(color_b, k), CHUNK)], l_sem.at[slot, 1]
            ),
        ]

    def dh_copy(i, v):
        return remote(dhbuf.at[part(vp)], dhbuf.at[part(vp)], v_sent.at[7 + i], v_got.at[7 + i], (dp, v))

    def gv_copy(i, v):
        return remote(gv.at[vp], gv.at[vp], v_sent.at[14 + i], v_got.at[14 + i], (dp, v))

    def gy_copy(i, d):
        return remote(gy.at[y], gy.at[y], v_sent.at[21 + i], v_got.at[21 + i], (d, vp))

    def gz_copy(i, d):
        return remote(gz.at[z], gz.at[z], v_sent.at[24 + i], v_got.at[24 + i], (d, vp))

    def total(buf, n):
        value = buf[0]
        for p in range(1, n):
            value += buf[p]
        return value

    def norm_backward():
        for i, v in enumerate(vs):
            source = lax.rem(vp + NV - 1 - i, NV)
            remote(dn_ref.at[part(v)], dnbuf.at[source], v_sent.at[i], v_got.at[i], (dp, v)).wait_recv()
        dnbuf[vp] = dn_ref[part(vp), :]
        d_normed = total(dnbuf, NV)
        x_hat, inv_std = rsqrt_norm(hid_ref[part(vp), :].astype(F32))
        value = d_normed * gain_ref[...]
        mean_one = jnp.mean(value, axis=-1, keepdims=True)
        mean_two = jnp.mean(value * x_hat, axis=-1, keepdims=True)
        dhbuf[part(vp), :] = (inv_std * (value - mean_one - x_hat * mean_two)).astype(BF16).astype(F32)
        gain_part = jnp.sum(d_normed * x_hat, axis=0, keepdims=True)
        gv[vp] = jnp.broadcast_to(gain_part, (8, WIDTH))
        for i, v in enumerate(vs):
            dh_copy(i, v).start()
            gv_copy(i, v).start()

    def hidden_out():
        for i, v in enumerate(vs):
            source = lax.rem(vp + NV - 1 - i, NV)
            place = dhbuf.at[part(source)]
            remote(place, place, v_sent.at[7 + i], v_got.at[7 + i], (dp, v)).wait_recv()
            remote(gv.at[source], gv.at[source], v_sent.at[14 + i], v_got.at[14 + i], (dp, v)).wait_recv()
        dh_ref[...] = dhbuf[...].astype(BF16)
        gy[y] = total(gv, NV)
        for i, d in enumerate(ys):
            gy_copy(i, d).start()

    def gain_y():
        for i, d in enumerate(ys):
            source = lax.rem(y + NY - 1 - i, NY)
            remote(gy.at[source], gy.at[source], v_sent.at[21 + i], v_got.at[21 + i], (d, vp)).wait_recv()
        gz[z] = total(gy, NY)
        for i, d in enumerate(zs):
            gz_copy(i, d).start()

    def gain_z():
        for i, d in enumerate(zs):
            source = lax.rem(z + NZ - 1 - i, NZ)
            remote(gz.at[source], gz.at[source], v_sent.at[24 + i], v_got.at[24 + i], (d, vp)).wait_recv()
        dg_ref[...] = total(gz, NZ)[0:1]

    def free(k, slot):
        for copy in out_copies(k, slot):
            copy.wait_send()
        for copy in keep_copies(k, slot):
            copy.wait()

    def chunk_step(k, carry):
        slot, rows_in = lax.rem(k, SLOTS), lax.rem(k, 2)
        for copy in fetch_rows(k, rows_in):
            copy.wait()

        @pl.when(k + 1 < NCHUNK)
        def _():
            for copy in fetch_rows(k + 1, 1 - rows_in):
                copy.start()

        @pl.when(k + 1 == NCHUNK)
        def _():
            fetch_rest(0, 1 - rows_in).start()

        @pl.when(k >= SLOTS)
        def _():
            free(k - SLOTS, slot)

        for step, work in ((1, norm_backward), (2, hidden_out), (3, gain_y), (4, gain_z)):
            pl.when(k == step)(work)

        acc[slot] = jnp.zeros((2 * CHUNK, WIDTH), F32)
        place = lax.broadcasted_iota(jnp.int32, (2 * CHUNK, 1), 0)
        ids = place + jnp.where(place < CHUNK, a_row(color_a, k), b_row(color_b, k) - CHUNK)

        def token_step(t, carry):
            @pl.when(k == 0)
            def _():
                half = lax.rem(t, 2)
                fetch_tokens(t, half).wait()

                @pl.when(t + 1 < NT)
                def _():
                    fetch_tokens(t + 1, 1 - half).start()

                nb[pl.ds(pl.multiple_of(t * TT, TT), TT), :] = stage[half].astype(BF16)

            block(slot, rows_in, t, 2 * CHUNK, ids)
            return carry

        lax.fori_loop(0, NT, token_step, 0)
        for copy in out_copies(k, slot) + keep_copies(k, slot):
            copy.start()
        return carry

    lax.fori_loop(0, NCHUNK, chunk_step, 0)

    rest_copies = []
    for p, (start, size) in enumerate(REST_PARTS):
        slot, rows_in = (NCHUNK + p) % SLOTS, (NCHUNK + p) % 2
        fetch_rest(p, rows_in).wait()
        if p + 1 < len(REST_PARTS):
            fetch_rest(p + 1, 1 - rows_in).start()
        free(NCHUNK + p - SLOTS, slot)
        acc[slot] = jnp.zeros((2 * CHUNK, WIDTH), F32)
        ids = lax.broadcasted_iota(jnp.int32, (size, 1), 0) + start

        def rest_step(t, carry):
            block(slot, rows_in, t, size, ids)
            return carry

        lax.fori_loop(0, NT, rest_step, 0)
        copy = pltpu.make_async_copy(acc.at[slot, pl.ds(0, size)], table_ref.at[pl.ds(start, size)], l_sem.at[slot, 0])
        copy.start()
        rest_copies.append(copy)

    free(NCHUNK - 1, (NCHUNK - 1) % SLOTS)
    for copy in rest_copies:
        copy.wait()

    def drain(k, carry):
        for copy in in_copies(k):
            copy.wait_recv()
        return carry

    lax.fori_loop(0, NCHUNK, drain, 0)
    for i, v in enumerate(vs):
        dn_copy(i, v).wait_send()
        dh_copy(i, v).wait_send()
        gv_copy(i, v).wait_send()
    for i, d in enumerate(ys):
        gy_copy(i, d).wait_send()
    for i, d in enumerate(zs):
        gz_copy(i, d).wait_send()


def table_grad(nall, stall, emb, dn, hidden, gain):
    any_space = pl.BlockSpec(memory_space=pl.ANY)
    vmem = pl.BlockSpec(memory_space=pltpu.VMEM)
    smem = pl.BlockSpec(memory_space=pltpu.SMEM)
    return pl.pallas_call(
        table_kernel,
        in_specs=[any_space, vmem, any_space, vmem, vmem, vmem],
        out_specs=[any_space, vmem, vmem, smem],
        out_shape=[
            jax.ShapeDtypeStruct((VLOC, WIDTH), F32),
            jax.ShapeDtypeStruct((TOK, WIDTH), BF16),
            jax.ShapeDtypeStruct((1, WIDTH), F32),
            jax.ShapeDtypeStruct((1, 1), F32),
        ],
        scratch_shapes=[
            pltpu.VMEM((NALL, WIDTH), BF16),
            pltpu.VMEM((2, TT, WIDTH), F32),
            pltpu.VMEM((2, 2 * CHUNK, WIDTH), BF16),
            pltpu.VMEM((SLOTS, 2 * CHUNK, WIDTH), F32),
            pltpu.VMEM((8, NALL), F32),
            pltpu.VMEM((NV, SLICE, WIDTH), F32),
            pltpu.VMEM((TOK, WIDTH), F32),
            pltpu.VMEM((NV, 8, WIDTH), F32),
            pltpu.VMEM((NY, 8, WIDTH), F32),
            pltpu.VMEM((NZ, 8, WIDTH), F32),
            pltpu.SemaphoreType.DMA((2,)),
            pltpu.SemaphoreType.DMA((2, 2)),
            pltpu.SemaphoreType.DMA((SLOTS, 2)),
            pltpu.SemaphoreType.DMA((SLOTS, 8)),
            pltpu.SemaphoreType.DMA((NCHUNK, 8)),
            pltpu.SemaphoreType.DMA((31,)),
            pltpu.SemaphoreType.DMA((31,)),
        ],
        compiler_params=pltpu.CompilerParams(
            collective_id=1, has_side_effects=True, vmem_limit_bytes=VMEM_LIMIT
        ),
        name="table_grad",
    )(nall, stall, emb, dn, hidden, gain)


def solution(mesh):
    def local_step(hidden, norm_gain, emb_table, labels, tok_mask):
        rows, seq_len, width = hidden.shape
        flat = hidden.reshape(rows * seq_len, width)
        gain = norm_gain.reshape(1, width)
        ids = jnp.stack([lax.axis_index("dp"), lax.axis_index("vp")]).astype(jnp.int32)
        nf, st = own_stats(ids[1:], flat, gain, labels.reshape(1, -1), tok_mask.reshape(1, -1), emb_table)
        nall, stall = gather(nf, st)
        dn = own_dn(ids, nf, stall, emb_table)
        table, d_hidden, d_gain, loss = table_grad(nall.reshape(NALL, width), stall, emb_table, dn, flat, gain)
        return loss[0, 0], table, d_hidden.reshape(rows, seq_len, width), d_gain[0]

    return jax.shard_map(
        local_step,
        mesh=mesh,
        in_specs=(P("dp", None, None), P(None), P("vp", None), P("dp", None), P("dp", None)),
        out_specs=(P(), P("vp", None), P("dp", None, None), P(None)),
        check_vma=False,
    )
```

time: 1370 us -> 610 us (0.45)
  waiting for transfers between devices: 1020 us -> 0 us
  Pallas kernels: 0 us -> 557 us
  blocking collectives: 170 us -> 0 us
  matrix products: 92.5 us -> 0 us
  other arithmetic: 24.1 us -> 1.93 us
  between operations: 17.3 us -> 2.48 us
    psum x2 -> x0, waiting for transfers between devices: 1020 us -> none  [the longest x1 1000 us: local_step(): lax.psum(jnp.einsum('tv,td->vd', d_logits, normed, preferred_element_type...]
    pallas_call x0 -> x4, Pallas kernels: none -> 557 us  [the longest x1 312 us: table_grad(): pl.pallas_call(table_kernel, in_specs=[any_space, vmem, any_space, vmem,...]
    psum x3 -> x0, blocking collectives: 143 us -> none  [the longest x1 65.3 us: local_step(): loss_sum = lax.psum(jnp.sum(flat_mask * (log_norm - label_logit)), 'dp')]
    dot_general x3 -> x0, matrix products: 92.5 us -> none  [the longest x1 37.2 us: local_step(): jnp.einsum('tv,td->vd', d_logits, normed, preferred_element_type=jnp.floa...]
    pmax x1 -> x0, blocking collectives: 26.8 us -> none  [local_step(): row_max = lax.pmax(jnp.max(logits, axis=1), 'vp')]
    reduce_sum x5 -> x0, other arithmetic: 19.5 us -> none  [the longest x1 13.5 us: local_step(): exp_sum = lax.psum(jnp.sum(shifted, axis=1), 'vp')]
    unnamed x9 -> x6, local copies, waits for them, and re-layouts: 43.9 us -> 47.3 us
  transfers between devices with their start and end apart: 2 -> 0, of which waited for: 2 -> 0; matrix products, arithmetic and copies ran while one was open for 3% -> 0% of each run, Pallas kernels for 0% -> 0%
where the time goes in v1:
time: 610 us; the launch traced here: 609 us
  Pallas kernels  557 us (91%)
  local copies, waits for them, and re-layouts  48.5 us (8%)
    pallas_call x1, Pallas kernels, table_grad(): pl.pallas_call(table_kernel, in_specs=[any_space, vmem, any_space, vmem,...  312 us
    pallas_call x1, Pallas kernels, gather(): pl.pallas_call(gather_kernel, in_specs=[vmem, vmem], out_specs=[any_space...  159 us
    pallas_call x1, Pallas kernels, own_dn(): pl.pallas_call(dn_kernel, grid_spec=pltpu.PrefetchScalarGridSpec(num_scal...  48.2 us
    unnamed x6, local copies, waits for them, and re-layouts  47.3 us
    pallas_call x1, Pallas kernels, own_stats(): pl.pallas_call(stats_kernel, grid_spec=pltpu.PrefetchScalarGridSpec(num_s...  37.1 us

profile of v1, /device:TPU:1, one launch (start us, length us, event | category | flops | bytes accessed | tf_op | source)
XLA Modules:
  0.0 609.5 jit_solution(13233702176085732511)
XLA Ops:
  0.6 0.6 pad_add_fusion.ids_ref
  1.3 1.2 copy.14
  2.5 1.3 copy.13
  3.8 1.3 reshape.27.gain_ref
  5.0 37.1 %own_stats.1 = (f32[384,896]{1,0:T(8,128)}, f32[8,384]{1,0:T(8,128)}) custom-call(s32[1]{0:T(128)} %bitcast.vp_ref, bf16[384,896]{1,0:T(8,128)(2,1)} %bitcast.17, f32[1,896]{1,0:T(1,128)} %reshape.27.gain_ref, s32[1,384]{1,0:T(1,128)} %bitcast.20, f32[1,384]{1,0:T(1,128)} %bitcast.21, bf16[18992,896]{1,0:T(8,128)(2,1)} %emb_ref.5), custom_call_target="tpu_custom_call" | custom-call | tf_op jit(solution)/shard_map/own_stats/pallas_call | solution.py:90
  42.1 158.9 %gather_tokens.1 = (f32[8,4,384,896]{3,2,1,0:T(8,128)}, f32[8,12288]{1,0:T(8,128)}) custom-call(f32[384,896]{1,0:T(8,128)} %get-tuple-element.12.nf_ref, f32[8,384]{1,0:T(8,128)} %get-tuple-element.13.st_ref), custom_call_target="tpu_custom_call" | custom-call | tf_op jit(solution)/shard_map/gather_tokens/pallas_call | solution.py:318
  201.0 48.2 %own_dn.1.dn_ref = f32[384,896]{1,0:T(8,128)} custom-call(s32[2]{0:T(128)} %pad_add_fusion.ids_ref, f32[384,896]{1,0:T(8,128)} %get-tuple-element.12.nf_ref, f32[8,12288]{1,0:T(8,128)} %get-tuple-element.15.st_ref.own_ref, f32[8,12288]{1,0:T(8,128)} %get-tuple-element.15.st_ref.own_ref, bf16[18992,896]{1,0:T(8,128)(2,1)} %emb_ref.5), custom_call_target="tpu_custom_call" | custom-call | tf_op jit(solution)/shard_map/own_dn/pallas_call | solution.py:364
  249.2 312.4 %table_grad.1 = (f32[18992,896]{1,0:T(8,128)}, bf16[384,896]{1,0:T(8,128)(2,1)}, f32[1,896]{1,0:T(1,128)}, f32[1,1]{1,0:T(1,128)}) custom-call(f32[12288,896]{1,0:T(8,128)} %bitcast.16, f32[8,12288]{1,0:T(8,128)} %get-tuple-element.15.st_ref.own_ref, bf16[18992,896]{1,0:T(8,128)(2,1)} %emb_ref.5, f32[384,896]{1,0:T(8,128)} %own_dn.1.dn_ref, ...), custom_call_target="tpu_custom_call" | custom-call | tf_op jit(solution)/shard_map/table_grad/pallas_call | solution.py:645
  561.6 1.3 reduce
  563.5 0.0 copy-start
  563.6 43.9 %copy.19 = f32[18992,896]{1,0:T(8,128)} copy(f32[18992,896]{1,0:T(8,128)} %get-tuple-element.25) | data formatting | bytes 136134656
  607.5 0.0 copy-done
  607.5 0.8 copy.20
Async XLA Ops:
  563.5 43.9 %copy-start = (bf16[384,896]{1,0:T(8,128)(2,1)S(1)}, bf16[384,896]{1,0:T(8,128)(2,1)}, u32[]{:S(2)}) copy-start(bf16[384,896]{1,0:T(8,128)(2,1)} %get-tuple-element.18) | copy-start | bytes 2064388

commit v2 on v0

v2 whole, which is shorter than its diff:
```python
import jax
import jax.numpy as jnp
from jax import lax
from jax.experimental import pallas as pl
from jax.experimental.pallas import tpu as pltpu
from jax.sharding import PartitionSpec as P

MESH = pl.DeviceIdType.MESH
LOGIT_SCALE = 0.0625
EPS = 1e-5
NZ, NY, NV = 8, 4, 8
NDP = NZ * NY
TOK, WIDTH, VLOC = 384, 896, 18992
NALL = NDP * TOK
F32, BF16 = jnp.float32, jnp.bfloat16

ROWS_0, ROWS_1 = 112, 144
Q_BASE = ROWS_0 + ROWS_1
Q_ROWS = (TOK - Q_BASE) // NY
Q_PART = TOK - Q_BASE

COLOR_ROWS, CHUNK = 2304, 192
HALF, PAIR = CHUNK // 2, 2 * CHUNK
NCHUNK = COLOR_ROWS // CHUNK
B_BASE = NY * COLOR_ROWS
REST_BASE = 2 * B_BASE
REST_PARTS = ((REST_BASE, 288), (REST_BASE + 288, VLOC - REST_BASE - 288))
SLOTS = 3

TT = 2048
NT = NALL // TT
TILE = NY * Q_BASE
NQ = NDP * Q_PART // TILE
VT, VPARTS = 1184, ((0, 304), (304, 304), (608, 288), (896, 288))
NVT = VLOC // VT
VTAIL = VLOC - NVT * VT
NSTEP = 2 * NVT
SLICE = TOK // NV


def dot_nt(a, b):
    return lax.dot_general(a, b, (((1,), (1,)), ((), ())), preferred_element_type=F32)


def rsqrt_norm(values):
    mean_x = jnp.mean(values, axis=-1, keepdims=True)
    centered = values - mean_x
    variance = jnp.mean(centered * centered, axis=-1, keepdims=True)
    inv_std = lax.rsqrt(variance + EPS)
    return centered * inv_std, inv_std


STEP = {"z+": (1, 0, 0), "z-": (-1, 0, 0), "y+": (0, 1, 0), "y-": (0, -1, 0), "x+": (0, 0, 1), "x-": (0, 0, -1)}


def add(msgs, link, z, y, rows, parents, q):
    msgs.append(dict(link=link, z=z, y=y, lo=rows[0], hi=rows[1], parents=parents, q=q))
    return [len(msgs) - 1]


def halves(lo, hi):
    return (lo, (lo + hi) // 2), ((lo + hi) // 2, hi)


def ring(msgs, whole, last, roots, q=None):
    added = []
    for link, half in zip(("z+", "z-"), last):
        parents = roots
        for s in range(1, NZ // 2 + 1):
            y, rows = whole if 2 * s < NZ else half
            parents = add(msgs, link, s * STEP[link][0], y, rows, parents, q)
            added += parents
    return added


def fan(msgs, whole, last, roots, q=None):
    added = []
    for link, half in zip(("y+", "y-"), last):
        dy = STEP[link][1]
        first = add(msgs, link, whole[0], dy, whole[1], roots, q)
        added += first
        if half is not None:
            added += add(msgs, link, half[0], 2 * dy, half[1], first, q)
    return added


def tree_first():
    msgs = []
    every = ((0, NZ // 2), (NZ // 2, NZ // 2))
    rows = (0, Q_ROWS)
    column = ring(msgs, (0, rows), [(0, part) for part in halves(*rows)], [], 0)
    up, up_half, down, down_half = fan(msgs, ((0, NZ), rows), [(part, rows) for part in every], column, 0)
    for y, roots in ((0, column), (1, [up]), (-1, [down]), (2, [up_half, down_half])):
        for link, part in zip(("x+", "x-"), every):
            dx = STEP[link][2]
            first = add(msgs, link, (0, NZ), y, rows, roots, dx)
            add(msgs, link, part, y, rows, first, 2 * dx)
    rows = (0, ROWS_0)
    own = fan(msgs, (0, rows), [(0, part) for part in halves(*rows)], [])
    every = ((0, NY // 2), (NY // 2, NY // 2))
    ring(msgs, ((0, NY), rows), [(part, rows) for part in every], column + own)
    return msgs


def tree_second():
    msgs = []
    rows = (ROWS_0, Q_BASE)
    parts = halves(*rows)
    nodes = ring(msgs, (0, rows), [(0, part) for part in parts], [])
    fan(msgs, (0, rows), [(0, part) for part in parts], [])
    for i in nodes:
        z, whole = msgs[i]["z"], (msgs[i]["lo"], msgs[i]["hi"])
        fan(msgs, (z, whole), [(z, part) if whole in (rows, part) else None for part in parts], [i])
    return msgs


def plane(m):
    return m["z"] % NZ if m["q"] is None else None


PLANES = [0] + [d for s in range(1, NZ // 2) for d in (s, NZ - s)] + [NZ // 2]
EARLY = NZ - 3
UNITS = PLANES[:EARLY] + [None] * NQ + PLANES[EARLY:]


def length(span):
    return span[1] if isinstance(span, tuple) else 1


def schedule(trees):
    tick, latency, rate, now = 0.25, 2.0, 88e3, 7.0
    queues = {(link, core): [] for link in STEP for core in range(2)}
    missing = [[set(m["parents"]) for m in msgs] for msgs in trees]
    arrived = [[] for _ in trees]
    taken = [[[] for _ in range(NSTEP + len(UNITS) + 1)] for _ in trees]

    def push(core, i):
        m = trees[core][i]
        size = (m["hi"] - m["lo"]) * length(m["z"]) * length(m["y"]) * WIDTH * 4
        queues[m["link"], core].append([i, size])

    def advance():
        for link in STEP:
            busy = [core for core in range(2) if queues[link, core]]
            for core in busy:
                head = queues[link, core][0]
                head[1] -= rate * tick / len(busy)
                if head[1] <= 0:
                    queues[link, core].pop(0)
                    arrived[core].append((now + latency, head[0]))
        return now + tick

    def collect(slot, limit):
        for core in range(2):
            for item in sorted(arrived[core]):
                if item[0] <= limit:
                    arrived[core].remove(item)
                    taken[core][slot].append(item[1])
                    for j, wants in enumerate(missing[core]):
                        if item[1] in wants:
                            wants.discard(item[1])
                            if not wants:
                                push(core, j)

    def lacking(wanted):
        return any(
            wanted(m) and not any(i in group for group in taken[core])
            for core, msgs in enumerate(trees)
            for i, m in enumerate(msgs)
        )

    for core, msgs in enumerate(trees):
        for i, m in enumerate(msgs):
            if not m["parents"]:
                push(core, i)
    end = now + latency
    for step in range(NSTEP):
        end += 1.65 if step < NVT else 2.7
        while now < end:
            now = advance()
        collect(step, now - 0.5)
        if step == NVT - 1:
            end += 4.0
    for u, d in enumerate(UNITS):
        while now < end or lacking(lambda m: plane(m) == d):
            now = advance()
            if now >= end:
                collect(NSTEP + u, now)
        end = now + 2.5
    while lacking(lambda m: True):
        now = advance()
        if now >= end:
            collect(NSTEP + len(UNITS), now)
    return taken, now


TREES = (tree_first(), tree_second())
TAKEN, GATHER_TIME = schedule(TREES)
NMSG = max(map(len, TREES))


def peers():
    dp, vp = lax.axis_index("dp"), lax.axis_index("vp")
    z, y = lax.div(dp, NY), lax.rem(dp, NY)
    ys = [z * NY + lax.rem(y + d, NY) for d in range(1, NY)]
    zs = [lax.rem(z + d, NZ) * NY + y for d in range(1, NZ)]
    vs = [lax.rem(vp + d, NV) for d in range(1, NV)]
    return dp, vp, z, y, ys, zs, vs


def greet(dp, vp, ys, zs, vs):
    barrier = pltpu.get_barrier_semaphore()
    everyone = [(d, vp) for d in ys + zs] + [(dp, v) for v in vs]
    for device in everyone:
        pl.semaphore_signal(barrier, inc=1, device_id=device, device_id_type=MESH)
    pl.semaphore_wait(barrier, len(everyone))


def remote(src, dst, send, recv, device):
    return pltpu.make_async_remote_copy(
        src_ref=src, dst_ref=dst, send_sem=send, recv_sem=recv, device_id=device, device_id_type=MESH
    )


def lanes(d, n=1):
    return pl.ds(pl.multiple_of(d * TOK, TOK), n * TOK)


def part(v):
    return pl.ds(pl.multiple_of(v * SLICE, SLICE), SLICE)


def total(buf, n):
    value = buf[0]
    for p in range(1, n):
        value += buf[p]
    return value


class Exchange:
    def __init__(self, sent, got, devices, me, place, source=None):
        self.count, self.me = len(devices), me
        self.make = lambda i, at, to: remote(source[i] if source and to else place(at), place(at), sent.at[i], got.at[i], devices[i])

    def start(self):
        for i in range(self.count):
            self.make(i, self.me, True).start()

    def wait(self):
        n = self.count + 1
        for i in range(self.count):
            self.make(i, lax.rem(self.me + n - 1 - i, n), False).wait_recv()

    def drain(self):
        for i in range(self.count):
            self.make(i, self.me, True).wait_send()


def step_kernel(
    hid_ref, gain_ref, lab_ref, mask_ref, emb_ref, table_ref, nall_ref, dh_ref, dg_ref, loss_ref,
    nf, own, vbuf, ebuf, tailbuf, m_s, s_s, l_s, stat, own_row, lsebuf, maskbuf, rows,
    nb, stage, cbuf, acc, planes, dn, dnbuf, dhbuf, gv, gy, gz,
    local, e_sem, sent, got, twin, stage_sem, c_sem, l_sem, row_sent, row_got,
    stat_sem, mask_y, mask_z, lse_y, lse_z, dn_sem, dh_sem, gv_sem, gy_sem, gz_sem,
):
    dp, vp, z, y, ys, zs, vs = peers()
    x, core = lax.div(vp, 2), lax.rem(vp, 2)
    other = vp + 1 - 2 * core
    y_devices = [(d, vp) for d in ys]
    z_devices = [(d, vp) for d in zs]
    v_devices = [(dp, v) for v in vs]

    def fetch(step, slot):
        start = pl.multiple_of(lax.rem(step, NVT) * VT, 16)
        return pltpu.make_async_copy(emb_ref.at[pl.ds(start, VT)], ebuf.at[slot], e_sem.at[slot])

    tail = pltpu.make_async_copy(emb_ref.at[pl.ds(NVT * VT, VTAIL)], tailbuf, local.at[2])
    fetch(0, 0).start()
    tail.start()
    greet(dp, vp, ys, zs, vs)

    gain = gain_ref[...].reshape(1, WIDTH)
    x_hat, _ = rsqrt_norm(hid_ref[...].astype(F32))
    normed = (gain * x_hat).astype(BF16)
    own[...] = normed
    nf[...] = normed.astype(F32)
    m_s[...] = jnp.full_like(m_s, -jnp.inf)
    s_s[...] = jnp.zeros_like(s_s)
    l_s[...] = jnp.zeros_like(l_s)
    dn[...] = jnp.zeros_like(dn)
    labels = jnp.concatenate([lab_ref[i : i + 1] for i in range(3)], axis=1)
    mask = jnp.concatenate([mask_ref[i : i + 1] for i in range(3)], axis=1)
    own_row[0:1] = labels.astype(F32)
    maskbuf[:, lanes(dp)] = jnp.concatenate([mask, labels.astype(F32), jnp.zeros((6, TOK), F32)], axis=0)

    def box_rows(m, dx=0):
        if m["q"] is None:
            return pl.ds(m["lo"], m["hi"] - m["lo"])
        start = Q_BASE + Q_ROWS * lax.rem(x - m["q"] + dx + NV, NY) + m["lo"]
        return pl.ds(pl.multiple_of(start, 8), m["hi"] - m["lo"])

    def region(m, dz=0, dy=0, dx=0):
        zz = pl.ds(*m["z"]) if isinstance(m["z"], tuple) else lax.rem(z - m["z"] + dz + 2 * NZ, NZ)
        yy = pl.ds(*m["y"]) if isinstance(m["y"], tuple) else lax.rem(y - m["y"] + dy + 2 * NY, NY)
        return nall_ref.at[zz, yy, box_rows(m, dx)]

    def target(link, back=False):
        dz, dy, dx = [-d if back else d for d in STEP[link]]
        row = lax.rem(z + dz + NZ, NZ) * NY + lax.rem(y + dy + NY, NY)
        return (row, lax.rem(vp + 2 * dx + NV, NV))

    def out_copy(msgs, i):
        m = msgs[i]
        there = region(m, *STEP[m["link"]])
        src = there if m["parents"] else nf.at[box_rows(m)]
        return remote(src, there, sent.at[i], got.at[i], target(m["link"]))

    def twin_copy(msgs, i):
        here = region(msgs[i])
        return remote(here, here, sent.at[NMSG + i], twin.at[i], (dp, other))

    def per_core(work):
        for which in range(2):
            pl.when(core == which)(lambda: work(which))

    def take(which, k):
        msgs = TREES[which]
        done = set(i for group in TAKEN[which][:k] for i in group)
        for i in TAKEN[which][k]:
            here = region(msgs[i])
            remote(here, here, sent.at[i], got.at[i], target(msgs[i]["link"], True)).wait_recv()
            done.add(i)
            for j, child in enumerate(msgs):
                if i in child["parents"] and done.issuperset(child["parents"]):
                    out_copy(msgs, j).start()
            twin_copy(msgs, i).start()

    def take_twins(which, wanted):
        msgs = TREES[1 - which]
        for group in TAKEN[1 - which]:
            for i in group:
                if wanted(msgs[i]):
                    twin_copy(msgs, i).wait_recv()

    def roots(which):
        for i, m in enumerate(TREES[which]):
            if not m["parents"]:
                out_copy(TREES[which], i).start()

    def drain_gather(which):
        for i in range(len(TREES[which])):
            out_copy(TREES[which], i).wait_send()
            twin_copy(TREES[which], i).wait_send()

    q_own = pl.ds(pl.multiple_of(Q_BASE + Q_ROWS * x, 8), Q_ROWS)
    keep_own = [
        pltpu.make_async_copy(nf.at[place], nall_ref.at[z, y, place], local.at[i])
        for i, place in enumerate((pl.ds(0, Q_BASE), q_own))
    ]
    per_core(roots)
    for copy in keep_own:
        copy.start()

    def spread(buf, y_sem, z_sem):
        to_y = Exchange(y_sem.at[0], y_sem.at[1], y_devices, y, lambda at: buf.at[:, lanes(z * NY + at)])
        to_z = Exchange(z_sem.at[0], z_sem.at[1], z_devices, z, lambda at: buf.at[:, lanes(at * NY, NY)])
        return to_y, to_z

    def turn(pair):
        pair[0].wait()
        pair[1].start()

    masks = spread(maskbuf, mask_y, mask_z)
    lses = spread(lsebuf, lse_y, lse_z)
    stats = Exchange(stat_sem.at[0], stat_sem.at[1], v_devices, vp, lambda at: vbuf.at[at])
    dns = Exchange(
        dn_sem.at[0], dn_sem.at[1], v_devices, vp, lambda at: dnbuf.at[at], [dn.at[part(v)] for v in vs]
    )
    dhs = Exchange(dh_sem.at[0], dh_sem.at[1], v_devices, vp, lambda at: dhbuf.at[part(at)])
    gvs = Exchange(gv_sem.at[0], gv_sem.at[1], v_devices, vp, lambda at: gv.at[at])
    gys = Exchange(gy_sem.at[0], gy_sem.at[1], y_devices, y, lambda at: gy.at[at])
    gzs = Exchange(gz_sem.at[0], gz_sem.at[1], z_devices, z, lambda at: gz.at[at])

    masks[0].start()
    for copy in (*keep_own, tail):
        copy.wait()

    def tile_ids(start, size):
        return lax.broadcasted_iota(jnp.int32, (size, 1), 0) + start

    def own_labels():
        return own_row[0:1].astype(jnp.int32) - vp * VLOC

    def stats_rows(carry, emb, start):
        m, s, picked = carry
        size = emb.shape[0]
        logits = LOGIT_SCALE * dot_nt(emb, own[...])
        groups = lambda value: value.reshape(size // 8, 8, TOK)
        top = jnp.maximum(m, jnp.max(groups(logits), axis=0))
        s = s * jnp.exp(m - top) + jnp.sum(jnp.exp(groups(logits) - top[None]), axis=0)
        hit = tile_ids(start, size) == own_labels()
        return top, s, picked + jnp.sum(groups(jnp.where(hit, logits, 0.0)), axis=0)

    def stats_step(tile, slot):
        carry = (m_s[...], s_s[...], l_s[...])
        for lo, size in VPARTS:
            carry = stats_rows(carry, ebuf[slot, lo : lo + size], tile * VT + lo)
        m_s[...], s_s[...], l_s[...] = carry

    def stats_send():
        m_s[...], s_s[...], l_s[...] = stats_rows((m_s[...], s_s[...], l_s[...]), tailbuf[...], NVT * VT)
        row_m = jnp.max(m_s[...], axis=0, keepdims=True)
        row_s = jnp.sum(s_s[...] * jnp.exp(m_s[...] - row_m), axis=0, keepdims=True)
        row_l = jnp.sum(l_s[...], axis=0, keepdims=True)
        vbuf[vp] = jnp.concatenate([row_m, row_s, row_l, jnp.zeros((5, TOK), F32)], axis=0)
        stats.start()

    def stats_join():
        stats.wait()
        row_m = vbuf[0, 0:1]
        for p in range(1, NV):
            row_m = jnp.maximum(row_m, vbuf[p, 0:1])
        row_s = jnp.zeros_like(row_m)
        row_l = jnp.zeros_like(row_m)
        for p in range(NV):
            row_s += vbuf[p, 1:2] * jnp.exp(vbuf[p, 0:1] - row_m)
            row_l += vbuf[p, 2:3]
        lse = row_m + jnp.log(row_s)
        lsebuf[:, lanes(dp)] = jnp.concatenate([lse, row_l, jnp.zeros((6, TOK), F32)], axis=0)
        own_row[1:2] = lse
        own_row[2:3] = maskbuf[0:1, lanes(dp)] * (LOGIT_SCALE / jnp.sum(maskbuf[0:1]))
        lses[0].start()

    def dn_rows(emb, start):
        soft = jnp.exp(LOGIT_SCALE * dot_nt(emb, own[...]) - own_row[1:2])
        hit = tile_ids(start, emb.shape[0]) == own_labels()
        d_logits = (jnp.where(hit, soft - 1.0, soft) * own_row[2:3]).astype(BF16)
        return lax.dot_general(d_logits, emb, (((0,), (0,)), ((), ())), preferred_element_type=F32)

    def dn_step(tile, slot):
        dn[...] += dn_rows(ebuf[slot], tile * VT)

    actions = {
        5: lambda: turn(masks),
        NVT - 2: lambda: masks[1].wait(),
        NVT - 1: stats_send,
        NVT + 8: lambda: turn(lses),
    }

    def compute_step(step, carry):
        slot = lax.rem(step, 2)
        fetch(step, slot).wait()

        @pl.when(step + 1 < NSTEP)
        def _():
            fetch(step + 1, 1 - slot).start()

        @pl.when(step < NVT)
        def _():
            stats_step(step, slot)

        @pl.when(step >= NVT)
        def _():
            dn_step(step - NVT, slot)

        for k in range(NSTEP):

            @pl.when(step == k)
            def _():
                if k in actions:
                    actions[k]()
                per_core(lambda which: take(which, k))
                if k == NVT - 1:
                    stats_join()

        return carry

    lax.fori_loop(0, NSTEP, compute_step, 0)
    dn[...] += dn_rows(tailbuf[...], NVT * VT)
    lses[1].wait()

    count = jnp.sum(maskbuf[0:1])
    loss_ref[0, 0] = jnp.sum(maskbuf[0:1] * (lsebuf[0:1] - lsebuf[1:2])) / count
    weight, local_label = maskbuf[0:1] * (LOGIT_SCALE / count), maskbuf[1:2] - (vp * VLOC).astype(F32)
    stat[...] = jnp.concatenate([lsebuf[0:1], weight, local_label, jnp.zeros((5, NALL), F32)], axis=0)
    for d in range(NDP):
        first, shared = d * Q_BASE, NDP * Q_BASE + d * Q_PART
        rows[:, first : first + Q_BASE] = stat[:, d * TOK : d * TOK + Q_BASE]
        rows[:, shared : shared + Q_PART] = stat[:, d * TOK + Q_BASE : (d + 1) * TOK]
    dns.start()

    color_a = lax.rem(y + 2 * z, NY)
    color_b = lax.rem(z + 2 * y, NY)

    def a_row(color, k, start=0):
        return pl.multiple_of(color * COLOR_ROWS + k * CHUNK + start, HALF)

    def b_row(color, k, start=0):
        return pl.multiple_of(B_BASE + color * COLOR_ROWS + k * CHUNK + start, HALF)

    def fetch_rows(k, slot):
        return [
            pltpu.make_async_copy(emb_ref.at[pl.ds(row, CHUNK)], cbuf.at[slot, pl.ds(i * CHUNK, CHUNK)], c_sem.at[slot, i])
            for i, row in enumerate((a_row(color_a, k), b_row(color_b, k)))
        ]

    def fetch_rest(p, slot):
        start, size = REST_PARTS[p]
        return pltpu.make_async_copy(emb_ref.at[pl.ds(start, size)], cbuf.at[slot, pl.ds(0, size)], c_sem.at[slot, 0])

    def chunk_ids(k):
        place = lax.broadcasted_iota(jnp.int32, (PAIR, 1), 0)
        return place + jnp.where(place < CHUNK, a_row(color_a, k), b_row(color_b, k) - CHUNK)

    def block(rows_in, start, tokens, ids):
        tok = pl.ds(pl.multiple_of(start, tokens), tokens)
        n = nb[tok, :]
        logits = LOGIT_SCALE * dot_nt(cbuf[rows_in, : ids.shape[0]], n)
        soft = jnp.exp(logits - rows[0:1, tok])
        hit = ids == rows[2:3, tok].astype(jnp.int32)
        d_logits = (jnp.where(hit, soft - 1.0, soft) * rows[1:2, tok]).astype(BF16)
        return jnp.dot(d_logits, n, preferred_element_type=F32)

    up_y, down_y = y_devices[0], y_devices[-1]
    up_z, down_z = z_devices[0], z_devices[-1]

    def row_copies(k, slot, a_from, b_from):
        plan = [
            (0, CHUNK, a_row(a_from[0], k), up_y),
            (0, CHUNK, a_row(a_from[1], k), down_y),
            (0, HALF, a_row(a_from[2], k), up_z),
            (HALF, HALF, a_row(a_from[3], k, HALF), down_z),
            (CHUNK, CHUNK, b_row(b_from[2], k), up_z),
            (CHUNK, CHUNK, b_row(b_from[3], k), down_z),
            (CHUNK, HALF, b_row(b_from[0], k), up_y),
            (CHUNK + HALF, HALF, b_row(b_from[1], k, HALF), down_y),
        ]
        return [
            remote(acc.at[slot, pl.ds(lo, n)], table_ref.at[pl.ds(row, n)], row_sent.at[slot, i], row_got.at[k, i], device)
            for i, (lo, n, row, device) in enumerate(plan)
        ]

    def out_copies(k, slot):
        return row_copies(k, slot, [color_a] * 4, [color_b] * 4)

    def in_copies(k):
        near_a = [lax.rem(color_a + d, NY) for d in (3, 1, 2, 2)]
        near_b = [lax.rem(color_b + d, NY) for d in (2, 2, 3, 1)]
        return row_copies(k, 0, near_a, near_b)

    def keep_copies(k, slot):
        return [
            pltpu.make_async_copy(acc.at[slot, pl.ds(i * CHUNK, CHUNK)], table_ref.at[pl.ds(row, CHUNK)], l_sem.at[slot, i])
            for i, row in enumerate((a_row(color_a, k), b_row(color_b, k)))
        ]

    def send_rows(k, slot):
        for copy in out_copies(k, slot) + keep_copies(k, slot):
            copy.start()

    def free(k, slot):
        for copy in out_copies(k, slot):
            copy.wait_send()
        for copy in keep_copies(k, slot):
            copy.wait()

    for k in range(2):
        for copy in fetch_rows(k, k):
            copy.start()
    for copy in fetch_rows(0, 0):
        copy.wait()
    first_ids = chunk_ids(0)

    def plane_of(u):
        p = jnp.where(u < EARLY, u, u - NQ)
        step = lax.div(p + 1, 2)
        return lax.rem(z + jnp.where(lax.rem(p, 2) == 1, NZ - step, step), NZ)

    def shared(u):
        return jnp.logical_and(u >= EARLY, u < EARLY + NQ)

    def tile_start(u):
        start = jnp.where(shared(u), NDP * Q_BASE + (u - EARLY) * TILE, plane_of(u) * TILE)
        return pl.multiple_of(start, TILE)

    def stage_plane(u):
        return [
            pltpu.make_async_copy(
                nall_ref.at[plane_of(u), i, pl.ds(0, Q_BASE)], stage.at[pl.ds(i * Q_BASE, Q_BASE)], stage_sem.at[i]
            )
            for i in range(NY)
        ]

    def stage_shared(u):
        per = TILE // Q_PART
        return [
            pltpu.make_async_copy(
                nall_ref.at[(u - EARLY) * (per // NY) + i // NY, i % NY, pl.ds(Q_BASE, Q_PART)],
                stage.at[pl.ds(i * Q_PART, Q_PART)],
                stage_sem.at[i],
            )
            for i in range(per)
        ]

    def each_stage(u, work):
        for is_it, copies in ((shared(u), stage_shared), (jnp.logical_not(shared(u)), stage_plane)):

            @pl.when(jnp.logical_and(is_it, u < len(UNITS)))
            def _():
                for copy in copies(u):
                    work(copy)

    acc[0] = jnp.zeros((PAIR, WIDTH), F32)

    def unit_step(u, carry):
        for k, d in enumerate(UNITS):

            @pl.when(u == k)
            def _():
                def arrive(which):
                    take(which, NSTEP + k)
                    if k == 0 or UNITS[k - 1] != d:
                        take_twins(which, lambda m: plane(m) == d)

                per_core(arrive)

        each_stage(u, lambda copy: copy.start())
        before = u - 1

        @pl.when(jnp.logical_and(u > 0, jnp.logical_not(shared(before))))
        def _():
            planes[plane_of(before)] = block(0, tile_start(before), TILE, first_ids)

        @pl.when(shared(before))
        def _():
            acc[0] += block(0, tile_start(before), TILE, first_ids)

        each_stage(u, lambda copy: copy.wait())

        @pl.when(u < len(UNITS))
        def _():
            nb[pl.ds(tile_start(u), TILE), :] = stage[...].astype(BF16)

        return carry

    lax.fori_loop(0, len(UNITS) + 1, unit_step, 0)
    per_core(lambda which: take(which, NSTEP + len(UNITS)))
    acc[0] += total(planes, NZ)
    send_rows(0, 0)

    def norm_backward():
        dns.wait()
        dnbuf[vp] = dn[part(vp), :]
        d_normed = total(dnbuf, NV)
        x_hat, inv_std = rsqrt_norm(hid_ref[part(vp), :].astype(F32))
        value = d_normed * gain_ref[...].reshape(1, WIDTH)
        mean_one = jnp.mean(value, axis=-1, keepdims=True)
        mean_two = jnp.mean(value * x_hat, axis=-1, keepdims=True)
        dhbuf[part(vp), :] = (inv_std * (value - mean_one - x_hat * mean_two)).astype(BF16).astype(F32)
        gv[vp] = jnp.broadcast_to(jnp.sum(d_normed * x_hat, axis=0, keepdims=True), (8, WIDTH))
        dhs.start()
        gvs.start()

    def hidden_out():
        dhs.wait()
        gvs.wait()
        dh_ref[...] = dhbuf[...].astype(BF16)
        gy[y] = total(gv, NV)
        gys.start()

    def gain_z():
        gys.wait()
        gz[z] = total(gy, NY)
        gzs.start()

    def gain_out():
        gzs.wait()
        dg_ref[...] = total(gz, NZ)[0:1].reshape(WIDTH)

    def chunk_step(k, carry):
        slot, rows_in = lax.rem(k, SLOTS), lax.rem(k, 2)
        for copy in fetch_rows(k, rows_in):
            copy.wait()

        @pl.when(k + 1 < NCHUNK)
        def _():
            for copy in fetch_rows(k + 1, 1 - rows_in):
                copy.start()

        @pl.when(k + 1 == NCHUNK)
        def _():
            fetch_rest(0, 1 - rows_in).start()

        @pl.when(k >= SLOTS)
        def _():
            free(k - SLOTS, slot)

        for when, work in ((1, norm_backward), (2, hidden_out), (5, gain_z), (9, gain_out)):
            pl.when(k == when)(work)

        acc[slot] = jnp.zeros((PAIR, WIDTH), F32)
        ids = chunk_ids(k)

        def token_step(t, carry):
            acc[slot] += block(rows_in, t * TT, TT, ids)
            return carry

        lax.fori_loop(0, NT, token_step, 0)
        send_rows(k, slot)
        return carry

    lax.fori_loop(1, NCHUNK, chunk_step, 0)

    rest_copies = []
    for p, (start, size) in enumerate(REST_PARTS):
        slot, rows_in = (NCHUNK + p) % SLOTS, (NCHUNK + p) % 2
        fetch_rest(p, rows_in).wait()
        if p + 1 < len(REST_PARTS):
            fetch_rest(p + 1, 1 - rows_in).start()
        free(NCHUNK + p - SLOTS, slot)
        acc[slot] = jnp.zeros((PAIR, WIDTH), F32)
        ids = lax.broadcasted_iota(jnp.int32, (size, 1), 0) + start

        def rest_step(t, carry):
            acc[slot, :size] += block(rows_in, t * TT, TT, ids)
            return carry

        lax.fori_loop(0, NT, rest_step, 0)
        copy = pltpu.make_async_copy(acc.at[slot, pl.ds(0, size)], table_ref.at[pl.ds(start, size)], l_sem.at[slot, 0])
        copy.start()
        rest_copies.append(copy)

    free(NCHUNK - 1, (NCHUNK - 1) % SLOTS)
    for copy in rest_copies:
        copy.wait()

    def drain_rows(k, carry):
        for copy in in_copies(k):
            copy.wait_recv()
        return carry

    lax.fori_loop(0, NCHUNK, drain_rows, 0)
    per_core(drain_gather)
    for exchange in (*masks, *lses, stats, dns, dhs, gvs, gys, gzs):
        exchange.drain()


def solution(mesh):
    def local_step(hidden, norm_gain, emb_table, labels, tok_mask):
        rows, seq_len, width = hidden.shape
        any_space = pl.BlockSpec(memory_space=pl.ANY)
        vmem = pl.BlockSpec(memory_space=pltpu.VMEM)
        smem = pl.BlockSpec(memory_space=pltpu.SMEM)
        v, sem = pltpu.VMEM, pltpu.SemaphoreType.DMA
        row8, wide8, block_f32 = v((8, TOK), F32), v((8, NALL), F32), v((TOK, WIDTH), F32)
        table, _, d_hidden, d_gain, loss = pl.pallas_call(
            step_kernel,
            in_specs=[vmem, vmem, vmem, vmem, any_space],
            out_specs=[any_space, any_space, vmem, vmem, smem],
            out_shape=[
                jax.ShapeDtypeStruct((VLOC, WIDTH), F32),
                jax.ShapeDtypeStruct((NZ, NY, TOK, WIDTH), F32),
                jax.ShapeDtypeStruct((TOK, WIDTH), BF16),
                jax.ShapeDtypeStruct((WIDTH,), F32),
                jax.ShapeDtypeStruct((1, 1), F32),
            ],
            scratch_shapes=[
                block_f32, v((TOK, WIDTH), BF16), v((NV, 8, TOK), F32), v((2, VT, WIDTH), BF16), v((VTAIL, WIDTH), BF16),
                row8, row8, row8, wide8, row8, wide8, wide8, wide8,
                v((NALL, WIDTH), BF16), v((TILE, WIDTH), F32), v((2, PAIR, WIDTH), BF16), v((SLOTS, PAIR, WIDTH), F32),
                v((NZ, PAIR, WIDTH), F32), block_f32, v((NV, SLICE, WIDTH), F32), block_f32,
                v((NV, 8, WIDTH), F32), v((NY, 8, WIDTH), F32), v((NZ, 8, WIDTH), F32),
                sem((3,)), sem((2,)), sem((2 * NMSG,)), sem((NMSG,)), sem((NMSG,)), sem((NZ,)), sem((2, 2)),
                sem((SLOTS, 2)), sem((SLOTS, 8)), sem((NCHUNK, 8)),
                sem((2, 7)), sem((2, 3)), sem((2, 7)), sem((2, 3)), sem((2, 7)),
                sem((2, 7)), sem((2, 7)), sem((2, 7)), sem((2, 3)), sem((2, 7)),
            ],
            compiler_params=pltpu.CompilerParams(
                collective_id=0, has_side_effects=True, vmem_limit_bytes=63 * 2**20 + 2**19
            ),
            name="head_step",
        )(hidden.reshape(rows * seq_len, width), norm_gain, labels, tok_mask, emb_table)
        return loss[0, 0], table, d_hidden.reshape(rows, seq_len, width), d_gain

    return jax.shard_map(
        local_step,
        mesh=mesh,
        in_specs=(P("dp", None, None), P(None), P("vp", None), P("dp", None), P("dp", None)),
        out_specs=(P(), P("vp", None), P("dp", None, None), P(None)),
        check_vma=False,
    )
```

time: 1370 us -> 482 us (0.35)
  waiting for transfers between devices: 1020 us -> 0 us
  Pallas kernels: 0 us -> 434 us
  blocking collectives: 170 us -> 0 us
  matrix products: 92.5 us -> 0 us
  other arithmetic: 24.1 us -> 0 us
  between operations: 17.3 us -> 2.42 us
    psum x2 -> x0, waiting for transfers between devices: 1020 us -> none  [the longest x1 1000 us: local_step(): lax.psum(jnp.einsum('tv,td->vd', d_logits, normed, preferred_element_type...]
    pallas_call x0 -> x1, Pallas kernels: none -> 434 us  [local_step(): pl.pallas_call(step_kernel, in_specs=[vmem, vmem, vmem, vmem, any_space],...]
    psum x3 -> x0, blocking collectives: 143 us -> none  [the longest x1 65.3 us: local_step(): loss_sum = lax.psum(jnp.sum(flat_mask * (log_norm - label_logit)), 'dp')]
    dot_general x3 -> x0, matrix products: 92.5 us -> none  [the longest x1 37.2 us: local_step(): jnp.einsum('tv,td->vd', d_logits, normed, preferred_element_type=jnp.floa...]
    pmax x1 -> x0, blocking collectives: 26.8 us -> none  [local_step(): row_max = lax.pmax(jnp.max(logits, axis=1), 'vp')]
    reduce_sum x5 -> x0, other arithmetic: 19.5 us -> none  [the longest x1 13.5 us: local_step(): exp_sum = lax.psum(jnp.sum(shifted, axis=1), 'vp')]
    unnamed x9 -> x7, local copies, waits for them, and re-layouts: 43.9 us -> 45.4 us
  transfers between devices with their start and end apart: 2 -> 0, of which waited for: 2 -> 0; matrix products, arithmetic and copies ran while one was open for 3% -> 0% of each run, Pallas kernels for 0% -> 0%
where the time goes in v2:
time: 482 us
  Pallas kernels  434 us (90%)
  local copies, waits for them, and re-layouts  45.4 us (9%)
    pallas_call x1, Pallas kernels, local_step(): pl.pallas_call(step_kernel, in_specs=[vmem, vmem, vmem, vmem, any_space],...  434 us
    unnamed x7, local copies, waits for them, and re-layouts  45.4 us

profile of v2, /device:TPU:1, one launch (start us, length us, event | category | flops | bytes accessed | tf_op | source)
XLA Modules:
  0.0 482.0 jit_solution(8155593974892530737)
XLA Ops:
  0.6 434.2 %head_step.1 = (f32[18992,896]{1,0:T(8,128)}, f32[8,4,384,896]{3,2,1,0:T(8,128)}, bf16[384,896]{1,0:T(8,128)(2,1)}, f32[896]{0:T(1024)}, f32[1,1]{1,0:T(1,128)}) custom-call(bf16[384,896]{1,0:T(8,128)(2,1)} %bitcast.4, f32[896]{0:T(1024)} %gain_ref.1, s32[3,128]{1,0:T(4,128)} %lab_ref.1, f32[3,128]{1,0:T(4,128)} %mask_ref.1, bf16[18992,896]{1,0:T(8,128)(2,1)} %emb_ref.1), custom_call_target="tpu_custom_call" | custom-call | tf_op jit(solution)/shard_map/head_step/pallas_call | solution.py:756
  435.5 0.0 copy-start
  435.5 0.0 copy-start.1
  435.5 43.9 %copy.14 = f32[18992,896]{1,0:T(8,128)} copy(f32[18992,896]{1,0:T(8,128)} %get-tuple-element.17) | data formatting | bytes 136134656
  479.4 0.0 copy-done
  479.4 0.8 copy.15
  480.3 0.0 copy-done.1
  480.3 0.6 copy.16
Async XLA Ops:
  435.5 43.9 %copy-start = (bf16[384,896]{1,0:T(8,128)(2,1)S(1)}, bf16[384,896]{1,0:T(8,128)(2,1)}, u32[]{:S(2)}) copy-start(bf16[384,896]{1,0:T(8,128)(2,1)} %get-tuple-element.10) | copy-start | bytes 2064388
  435.5 44.8 %copy-start.1 = (f32[896]{0:T(1024)S(1)}, f32[896]{0:T(1024)}, u32[]{:S(2)}) copy-start(f32[896]{0:T(1024)} %get-tuple-element.19) | copy-start | bytes 10756
